TPU v7x, 32 devices: a whole 2x2x4 slice. The times are simulated.
32 devices in a mesh: groups: 2 (over x), blk: 16 (over z, y, core).
Axes of the slice: x: 2, y: 2, z: 4, core: 2. Of those that a mesh axis runs over, the one named last changes fastest.
Arguments:
- coords: float32 [32, 24576], P(None, ('groups', 'blk')), parts along dimension 1, may hold values from -6 to 6
- alpha: float32 [24576], P(('groups', 'blk')), parts along dimension 0, may hold values from -6 to 6
- probe_solves: float32 [15, 24576], P(None, ('groups', 'blk')), parts along dimension 1, may hold values from -6 to 6
- probes: float32 [15, 24576], P(None, ('groups', 'blk')), parts along dimension 1, may hold values from -6 to 6
- lengthscale: float32 [32], replicated, may hold values from 4 to 12
Outputs:
- grad: float32 [32, 24576], P(None, ('groups', 'blk')), parts along dimension 1
There are 2 independent parts, one for each index of `groups`. A program takes and returns all parts, laid end to end along the dimension named above; an argument that names none is the same for every part. Nothing has to cross between parts.
All inputs are finite; a program needn't handle non-finite values.
Results may differ from a plain program's by a relative error of at most 0.00014.
Values sent between devices are 32-bit elements; how exact they have to be, the bound alone decides.
A program may use at most 64 MiB of HBM per device.

v0:
```python
import functools
import math

import jax
import jax.numpy as jnp
from jax import lax
from jax.experimental import pallas as pl
from jax.experimental.pallas import tpu as pltpu
from jax.sharding import PartitionSpec as P

unit = 5.0**0.5 * math.log2(math.e)
ln_two = math.log(2.0)
inv_ln_two = 1.0 / ln_two
f32, bf16 = jnp.float32, jnp.bfloat16
piece = 256


def pieces(x):
    high = x.astype(bf16)
    rest = x - high.astype(f32)
    mid = rest.astype(bf16)
    low = (rest - mid.astype(f32)).astype(bf16)
    return high, mid, low


def norm_rows(field, own):
    high, mid, low = (p.astype(f32) for p in pieces(jnp.sum(field * field, 0, keepdims=True)))
    row = lax.broadcasted_iota(jnp.int32, (16, field.shape[1]), 0)
    first = 0 if own else 3
    ones = (row >= 3 - first) & (row < 6 - first)
    out = jnp.where(ones, 1.0, 0.0)
    for at, piece in enumerate((high, mid, low)):
        out = jnp.where(row == first + at, piece, out)
    return out.astype(bf16)


def kernel(
    dims, steps, count, coords, alpha, solves, probes, lengths, out,
    msg, recv, left_d, left_c, right_d, right_c, acc, send_sem, recv_sem,
):
    me = lax.axis_index("blk")
    core = lax.rem(me, 2)
    side = lax.rem(me // 2, 2)
    partner = {"blk": me + 1 - 2 * core}
    mate = {"blk": me + 2 - 4 * side}
    rows, block = msg.shape
    width = (rows - dims) // 2
    msg[:dims, :] = coords[...]
    line = alpha[...].reshape(1, block)
    msg[dims : dims + width, :] = jnp.concatenate([solves[...], line], 0)
    msg[dims + width :, :] = jnp.concatenate([probes[...], jnp.zeros_like(line)], 0)

    def at(offset):
        return {"blk": lax.rem(me + offset + count, count)}

    offsets = [sign * k for k in range(4, steps + 1, 4) for sign in (1, -1)]
    straight = {k: i for i, k in enumerate(offsets)}
    straights = len(offsets)
    rails = 2 * straights
    barrier = pltpu.get_barrier_semaphore()
    devices = [at(k) for k in offsets] + [mate, partner]
    for device in devices:
        pl.semaphore_signal(barrier, inc=1, device_id=device, device_id_type=pl.DeviceIdType.MESH)
    pl.semaphore_wait(barrier, len(devices))

    copies = {}
    parts = block // piece

    def send(src, slot, part, device):
        columns = pl.ds(part * piece, piece)
        copy = pltpu.make_async_remote_copy(
            src_ref=src.at[:, columns],
            dst_ref=recv.at[slot, :, columns],
            send_sem=send_sem.at[slot, part],
            recv_sem=recv_sem.at[slot, part],
            device_id=device,
            device_id_type=pl.DeviceIdType.MESH,
        )
        copy.start()
        copies[slot, part] = copy

    def arrive(slot, part):
        copies[slot, part].wait_recv()

    for part in range(parts):
        send(msg, rails, part, partner)
        for k in offsets:
            send(msg, straight[-k], part, at(k))
        send(msg, straights, part, mate)

    dim = lax.broadcasted_iota(jnp.int32, (dims, 128), 0)
    length = jnp.full((dims, 128), 1.0, f32)
    for d in range(dims):
        length = jnp.where(dim == d, lengths[d], length)
    length = length[:, :1]
    inverse = unit / length

    field = msg[:dims, :] * inverse
    high, mid, low = pieces(-2.0 * field)
    left_d[...] = jnp.concatenate([high, high, high, norm_rows(field, True), mid, mid, low], 0).T
    row = lax.broadcasted_iota(jnp.int32, (width, block), 0)
    scale = -ln_two / (2.0 * (width - 1))
    top, bottom = msg[dims : dims + width, :], msg[dims + width :, :]
    first = jnp.where(row == width - 1, ln_two * top, scale * bottom)
    second = jnp.where(row == width - 1, 0.0, scale * top)
    high, mid, low = pieces(jnp.concatenate([first, second], 0))
    left_c[...] = jnp.concatenate([high, high, high, mid, mid, low], 0).T

    done = [0]

    def visit(slot, part):
        buffer, fresh = done[0] % 2, done[0] == 0
        done[0] += 1
        columns = pl.ds(part * piece, piece)
        field = recv[slot, :dims, columns] * inverse
        high, mid, low = pieces(field)
        right_d[buffer] = jnp.concatenate([high, mid, low, norm_rows(field, False), high, mid, high], 0)
        table = recv[slot, dims:, columns]
        high, mid, low = pieces(table)
        right_c[buffer] = jnp.concatenate([high, mid, low, high, mid, high], 0)
        across = right_d[buffer, : 3 * dims + 16, :]
        for start in (0,):
            lines = pl.ds(start, block)
            distance = jnp.dot(left_d[lines, :], right_d[buffer], preferred_element_type=f32)
            coupling = jnp.dot(left_c[lines, :], right_c[buffer], preferred_element_type=f32)
            distance = jnp.maximum(distance, 1e-30)
            radius = distance * lax.rsqrt(distance)
            weighted = coupling * ((radius + inv_ln_two) * jnp.exp2(-radius))
            w_high = weighted.astype(bf16)
            w_low = (weighted - w_high.astype(f32)).astype(bf16)
            contract = (((1,), (1,)), ((), ()))
            part_sum = lax.dot_general(w_high, across, contract, preferred_element_type=f32)
            part_sum += lax.dot_general(w_low, across, contract, preferred_element_type=f32)
            if fresh and part == 0:
                acc[lines, :] = part_sum
            else:
                acc[lines, :] += part_sum

    every = range(parts)
    for part in every:
        arrive(rails, part)
        visit(rails, part)

    mated, crossed = straights, rails
    for k in range(4, steps + 1, 4):
        plus, minus = straight[k], straight[-k]
        last = k == steps
        for part in every:
            if k == 4:
                arrive(straights, part)
                send(recv.at[straights], rails + 1, part, partner)
                visit(straights, part)
            arrive(plus, part)
            arrive(minus, part)
            if last:
                send(recv.at[plus + side], straights + 1 + plus, part, mate)
                send(recv.at[plus + core], rails + 2 + plus, part, partner)
            else:
                for slot in (plus, minus):
                    send(recv.at[slot], straights + 1 + slot, part, mate)
                    send(recv.at[slot], rails + 2 + slot, part, partner)
            if k == 4:
                arrive(rails + 1, part)
                visit(rails + 1, part)
            visit(plus, part)
            visit(minus, part)
    ends = rails + 1 + straights
    for slot in range(straights + 1, rails):
        for part in every:
            arrive(slot, part)
            send(recv.at[slot], ends + slot - straights - 1, part, partner)
            arrive(rails + 1 + slot - straights, part)
            visit(rails + 1 + slot - straights, part)
            visit(slot, part)
    for slot in range(ends, 2 * rails):
        for part in every:
            arrive(slot, part)
            visit(slot, part)
    total = acc[...].T
    moved = total[:dims] + total[dims : 2 * dims] + total[2 * dims : 3 * dims]
    field = msg[:dims, :] * inverse
    out[...] = (-(5.0 / 3.0) / unit / length) * (field * total[3 * dims : 3 * dims + 1] - moved)
    for copy in copies.values():
        copy.wait_send()


def on_device(coords, alpha, probe_solves, probes, lengthscale):
    count = lax.axis_size("blk")
    steps = count // 4
    dims, block = coords.shape
    table_rows = 2 * (probes.shape[0] + 1)
    rows = dims + table_rows
    depth_d, depth_c = 6 * dims + 16, 6 * table_rows
    parts = block // piece
    return pl.pallas_call(
        functools.partial(kernel, dims, steps, count),
        out_shape=jax.ShapeDtypeStruct((dims, block), f32),
        in_specs=[pl.BlockSpec(memory_space=pltpu.VMEM)] * 4 + [pl.BlockSpec(memory_space=pltpu.SMEM)],
        out_specs=pl.BlockSpec(memory_space=pltpu.VMEM),
        scratch_shapes=[
            pltpu.VMEM((rows, block), f32),
            pltpu.VMEM((2 * steps, rows, block), f32),
            pltpu.VMEM((block, depth_d), bf16),
            pltpu.VMEM((block, depth_c), bf16),
            pltpu.VMEM((2, depth_d, piece), bf16),
            pltpu.VMEM((2, depth_c, piece), bf16),
            pltpu.VMEM((block, 3 * dims + 16), f32),
            pltpu.SemaphoreType.DMA((2 * steps, parts)),
            pltpu.SemaphoreType.DMA((2 * steps, parts)),
        ],
        compiler_params=pltpu.CompilerParams(collective_id=0, has_side_effects=True),
    )(coords, alpha, probe_solves, probes, lengthscale)


def solution(mesh):
    return jax.shard_map(
        on_device,
        mesh=mesh,
        in_specs=(
            P(None, ("groups", "blk")),
            P(("groups", "blk")),
            P(None, ("groups", "blk")),
            P(None, ("groups", "blk")),
            P(),
        ),
        out_specs=P(None, ("groups", "blk")),
        check_vma=False,
    )
```

profile of v0, /device:TPU:0, one launch (start us, length us, event | category | flops | bytes accessed | tf_op | source)
XLA Modules:
  0.0 27.3 jit_solution(8077684097401309976)
XLA Ops:
  0.0 25.8 %shard_map.55 = f32[32,768]{1,0:T(8,128)} custom-call(f32[32,768]{1,0:T(8,128)} %coords.1, f32[768]{0:T(1024)} %alpha.1, f32[15,768]{1,0:T(8,128)} %solves.1, f32[15,768]{1,0:T(8,128)} %probes.1, f32[32]{0:T(128)} %lengths.1), custom_call_target="tpu_custom_call" | custom-call | tf_op jit(solution)/shard_map/pallas_call | solution.py:195
  25.8 1.5 %copy.7 = f32[32,768]{1,0:T(8,128)} copy(f32[32,768]{1,0:T(8,128)} %shard_map.55) | data formatting | bytes 196608
where the time goes:
time: 27.6 us; the launch traced here: 27.3 us
  Pallas kernels  25.8 us (93%)
  local copies, waits for them, and re-layouts  1.54 us (6%)
    pallas_call x1, Pallas kernels, on_device(): pl.pallas_call(functools.partial(kernel, dims, steps, count), out_shape=j...  25.8 us
    unnamed x1, local copies, waits for them, and re-layouts  1.54 us

commit v1 on v0

v1 whole, which is shorter than its diff:
```python
import functools
import math

import jax
import jax.numpy as jnp
from jax import lax
from jax.experimental import pallas as pl
from jax.experimental.pallas import tpu as pltpu
from jax.sharding import PartitionSpec as P

unit = 5.0**0.5 * math.log2(math.e)
ln_two = math.log(2.0)
inv_ln_two = 1.0 / ln_two
f32, bf16 = jnp.float32, jnp.bfloat16
piece, chunk = 256, 256


def pieces(x):
    high = x.astype(bf16)
    rest = x - high.astype(f32)
    mid = rest.astype(bf16)
    low = (rest - mid.astype(f32)).astype(bf16)
    return high, mid, low


def norm_rows(field, own):
    high, mid, low = (p.astype(f32) for p in pieces(jnp.sum(field * field, 0, keepdims=True)))
    row = lax.broadcasted_iota(jnp.int32, (16, field.shape[1]), 0)
    first = 0 if own else 3
    ones = (row >= 3 - first) & (row < 6 - first)
    out = jnp.where(ones, 1.0, 0.0)
    for at, piece in enumerate((high, mid, low)):
        out = jnp.where(row == first + at, piece, out)
    return out.astype(bf16)


def kernel(
    dims, steps, count, coords, alpha, solves, probes, lengths, out,
    msg, line, held, held2, scales, recv, left_d, left_c, right_d, right_c, hold_d, hold_c, acc, load_sem, ready, send_sem, recv_sem,
):
    me = lax.axis_index("blk")
    core = lax.rem(me, 2)
    side = lax.rem(me // 2, 2)
    parts, rows, _ = msg.shape
    block = parts * piece
    width = (rows - dims) // 2

    def at(offset):
        return {"blk": lax.rem(me + offset + count, count)}

    partner = {"blk": me + 1 - 2 * core}
    mate = {"blk": me + 2 - 4 * side}
    reaches = range(4, steps + 1, 4)
    barrier = pltpu.get_barrier_semaphore()
    flip = 1 - 2 * side
    devices = [at(flip * k) for k in reaches] + [mate, partner]
    for device in devices:
        pl.semaphore_signal(barrier, inc=1, device_id=device, device_id_type=pl.DeviceIdType.MESH)

    loads = [(coords.at[:, pl.ds(p * piece, piece)], msg.at[p, pl.ds(0, dims), :]) for p in range(block // piece)]
    loads += [
        (solves, held),
        (probes, held2),
        (alpha, line),
        (lengths, scales),
    ]
    loads = [pltpu.make_async_copy(src, dst, load_sem.at[i]) for i, (src, dst) in enumerate(loads)]
    for load in loads:
        load.start()
    for load in loads:
        load.wait()
    extra = line[...].reshape(1, block)
    table = jnp.concatenate([held[...], extra, held2[...], jnp.zeros_like(extra)], 0)
    for p in range(parts):
        msg[p, dims:, :] = table[:, p * piece : (p + 1) * piece]
    pl.semaphore_wait(barrier, len(devices))

    copies = {}
    names = []

    def slot(name):
        if name not in names:
            names.append(name)
        return names.index(name)

    def send(src, name, part, device, now=True):
        copy = pltpu.make_async_remote_copy(
            src_ref=src.at[part],
            dst_ref=recv.at[slot(name), part],
            send_sem=send_sem.at[slot(name), part],
            recv_sem=recv_sem.at[slot(name), part],
            device_id=device,
            device_id_type=pl.DeviceIdType.MESH,
        )
        if now:
            copy.start()
        copies[name, part] = copy

    def arrive(name, part):
        copies[name, part].wait_recv()

    every = range(parts)

    def toward(name, k, part):
        send(msg, (name, k), part, at(-flip * k if name == "urgent" else flip * k))

    for i, k in enumerate(reaches):
        pl.semaphore_signal(ready.at[i], inc=1, device_id=at(-flip * k), device_id_type=pl.DeviceIdType.MESH)
    for part in every:
        for k in reaches:
            toward("urgent", k, part)
        send(msg, "mate", part, mate)
        send(msg, "partner", part, partner)
    dim = lax.broadcasted_iota(jnp.int32, (dims, 128), 0)
    length = jnp.full((dims, 128), 1.0, f32)
    for d in range(dims):
        length = jnp.where(dim == d, scales[d], length)
    length = length[:, :1]
    inverse = unit / length

    whole = jnp.concatenate([msg[p] for p in range(parts)], 1)
    field = whole[:dims, :] * inverse
    high, mid, low = pieces(-2.0 * field)
    left_d[...] = jnp.concatenate([high, high, high, norm_rows(field, True), mid, mid, low], 0).T
    row = lax.broadcasted_iota(jnp.int32, (width, block), 0)
    scale = math.e * ln_two / (2.0 * (width - 1))
    top, bottom = whole[dims : dims + width, :], whole[dims + width :, :]
    first = jnp.where(row == width - 1, -math.e * ln_two * top, scale * bottom)
    second = jnp.where(row == width - 1, 0.0, scale * top)
    high, mid, low = pieces(jnp.concatenate([first, second], 0))
    left_c[...] = jnp.concatenate([high, high, high, mid, mid, low], 0).T

    done = []
    pending = []
    contract = (((1,), (1,)), ((), ()))

    def finish(distance, coupling, buffer, lines, fresh):
        distance = jnp.maximum(distance, 1e-30)
        radius = distance * lax.rsqrt(distance)
        power = -inv_ln_two - radius
        weighted = coupling * power * jnp.exp2(power)
        w_high = weighted.astype(bf16)
        w_low = (weighted - w_high.astype(f32)).astype(bf16)
        across = right_d[buffer, : 3 * dims + 16, :]
        part_sum = lax.dot_general(across, w_high, contract, preferred_element_type=f32)
        part_sum += lax.dot_general(across, w_low, contract, preferred_element_type=f32)
        if fresh:
            acc[:, lines] = part_sum
        else:
            acc[:, lines] += part_sum

    def settle():
        if pending:
            finish(hold_d[...], hold_c[...], *pending.pop())

    def visit(*tiles):
        settle()
        for name, part in tiles:
            buffer, fresh = len(done) % 2, not done
            done.append(0)
            field = recv[slot(name), part, :dims, :] * inverse
            high, mid, low = pieces(field)
            right_d[buffer] = jnp.concatenate([high, mid, low, norm_rows(field, False), high, mid, high], 0)
            table = recv[slot(name), part, dims:, :]
            high, mid, low = pieces(table)
            right_c[buffer] = jnp.concatenate([high, mid, low, high, mid, high], 0)
            for start in range(0, block, chunk):
                lines = pl.ds(start, chunk)
                distance = jnp.dot(left_d[lines, :], right_d[buffer], preferred_element_type=f32)
                coupling = jnp.dot(left_c[lines, :], right_c[buffer], preferred_element_type=f32)
                if start + chunk == block and (name, part) == tiles[-1]:
                    hold_d[...] = distance
                    hold_c[...] = coupling
                    pending.append((buffer, lines, fresh))
                else:
                    finish(distance, coupling, buffer, lines, fresh)

    def land(name, part, onward=None, device=None, source=None):
        arrive(name, part)
        if onward is not None:
            send(recv.at[slot(name) if source is None else source], onward, part, device)

    for part in every:
        land("partner", part)
    visit(*[("partner", part) for part in every])
    for i, k in enumerate(reaches):
        pl.semaphore_wait(ready.at[i], 1)
        for part in every:
            toward("plain", k, part)

    last = steps
    inner = [(name, k) for k in reaches if k < last for name in ("urgent", "plain")]
    urgent, plain = ("urgent", last), ("plain", last)
    cross = jnp.where(core == side, slot(urgent), slot(plain))
    for part in every:
        land("mate", part, "mate2", partner)
        visit(("mate", part))
    for part in every:
        land(urgent, part, "over", mate)
        land("mate2", part)
        visit(("mate2", part), (urgent, part))
    for one in inner:
        for part in every:
            land(one, part, ("over", one), mate)
            send(recv.at[slot(one)], ("core", one), part, partner)
            visit((one, part))
    for part in every:
        land(plain, part, "cross", partner, cross)
        land("over", part, "over2", partner)
        visit((plain, part), ("over", part))
    for one in inner:
        for part in every:
            land(("over", one), part, ("over2", one), partner)
            land(("core", one), part)
            visit((("over", one), part), (("core", one), part))
            land(("over2", one), part)
            visit((("over2", one), part))
    for part in every:
        land("cross", part)
        land("over2", part)
        visit(("cross", part), ("over2", part))
    settle()
    total = acc[...]
    moved = total[:dims] + total[dims : 2 * dims] + total[2 * dims : 3 * dims]
    field = jnp.concatenate([msg[p, :dims, :] for p in range(parts)], 1) * inverse
    out[...] = (-(5.0 / 3.0) / unit / length) * (field * total[3 * dims : 3 * dims + 1] - moved)
    for copy in copies.values():
        copy.wait_send()


def on_device(coords, alpha, probe_solves, probes, lengthscale):
    count = lax.axis_size("blk")
    steps = count // 4
    dims, block = coords.shape
    table_rows = 2 * (probes.shape[0] + 1)
    rows = dims + table_rows
    depth_d, depth_c = 6 * dims + 16, 6 * table_rows
    parts = block // piece
    return pl.pallas_call(
        functools.partial(kernel, dims, steps, count),
        out_shape=pltpu.VMEM((dims, block), f32),
        in_specs=[pl.BlockSpec(memory_space=pltpu.HBM)] * 5,
        out_specs=pl.BlockSpec(memory_space=pltpu.VMEM),
        scratch_shapes=[
            pltpu.VMEM((parts, rows, piece), f32),
            pltpu.VMEM((block,), f32),
            pltpu.VMEM(probes.shape, f32),
            pltpu.VMEM(probes.shape, f32),
            pltpu.SMEM((dims,), f32),
            pltpu.VMEM((2 * steps, parts, rows, piece), f32),
            pltpu.VMEM((block, depth_d), bf16),
            pltpu.VMEM((block, depth_c), bf16),
            pltpu.VMEM((2, depth_d, piece), bf16),
            pltpu.VMEM((2, depth_c, piece), bf16),
            pltpu.VMEM((chunk, piece), f32),
            pltpu.VMEM((chunk, piece), f32),
            pltpu.VMEM((3 * dims + 16, block), f32),
            pltpu.SemaphoreType.DMA((parts + 4,)),
            pltpu.SemaphoreType.REGULAR((steps // 4,)),
            pltpu.SemaphoreType.DMA((2 * steps, parts)),
            pltpu.SemaphoreType.DMA((2 * steps, parts)),
        ],
        compiler_params=pltpu.CompilerParams(collective_id=0, has_side_effects=True),
    )(coords, alpha, probe_solves, probes, lengthscale)


def solution(mesh):
    return jax.shard_map(
        on_device,
        mesh=mesh,
        in_specs=(
            P(None, ("groups", "blk")),
            P(("groups", "blk")),
            P(None, ("groups", "blk")),
            P(None, ("groups", "blk")),
            P(),
        ),
        out_specs=P(None, ("groups", "blk")),
        check_vma=False,
    )
```

time: 27.6 us -> 23 us (0.83)
  Pallas kernels: 25.8 us -> 22.1 us
  local copies, waits for them, and re-layouts: 1.54 us -> 0.64 us
    pallas_call x1, Pallas kernels: 25.8 us -> 22.1 us  [on_device(): pl.pallas_call(functools.partial(kernel, dims, steps, count), out_shape=p...]
    unnamed x1, local copies, waits for them, and re-layouts: 1.54 us -> 0.64 us
where the time goes in v1:
time: 23 us; the launch traced here: 22.8 us
  Pallas kernels  22.1 us (96%)
  local copies, waits for them, and re-layouts  0.64 us (3%)
    pallas_call x1, Pallas kernels, on_device(): pl.pallas_call(functools.partial(kernel, dims, steps, count), out_shape=p...  22.1 us
    unnamed x1, local copies, waits for them, and re-layouts  0.64 us

profile of v1, /device:TPU:0, one launch (start us, length us, event | category | flops | bytes accessed | tf_op | source)
XLA Modules:
  0.0 22.8 jit_solution(15611022050790243358)
XLA Ops:
  0.0 22.1 %shard_map.55 = f32[32,768]{1,0:T(8,128)S(1)} custom-call(f32[32,768]{1,0:T(8,128)} %coords.1, f32[768]{0:T(1024)} %alpha.1, f32[15,768]{1,0:T(8,128)} %solves.1, f32[15,768]{1,0:T(8,128)} %probes.1, f32[32]{0:T(128)} %lengths.1), custom_call_target="tpu_custom_call" | custom-call | tf_op jit(solution)/shard_map/pallas_call | solution.py:239
  22.1 0.6 %copy.7 = f32[32,768]{1,0:T(8,128)} copy(f32[32,768]{1,0:T(8,128)S(1)} %shard_map.55) | data formatting | bytes 196608

commit v2 on v1

--- a/solution.py
+++ b/solution.py
@@ -12,7 +12,7 @@
 ln_two = math.log(2.0)
 inv_ln_two = 1.0 / ln_two
 f32, bf16 = jnp.float32, jnp.bfloat16
-piece, chunk = 256, 256
+piece, chunk = 256, 128
 
 
 def pieces(x):
@@ -36,7 +36,7 @@
 
 def kernel(
     dims, steps, count, coords, alpha, solves, probes, lengths, out,
-    msg, line, held, held2, scales, recv, left_d, left_c, right_d, right_c, hold_d, hold_c, acc, load_sem, ready, send_sem, recv_sem,
+    msg, line, held, held2, scales, recv, left_d, left_c, right_d, right_c, hold_d, hold_c, acc, load_sem, send_sem, recv_sem,
 ):
     me = lax.axis_index("blk")
     core = lax.rem(me, 2)
@@ -53,7 +53,7 @@
     reaches = range(4, steps + 1, 4)
     barrier = pltpu.get_barrier_semaphore()
     flip = 1 - 2 * side
-    devices = [at(flip * k) for k in reaches] + [mate, partner]
+    devices = [at(sign * k) for k in reaches for sign in (1, -1)] + [mate, partner]
     for device in devices:
         pl.semaphore_signal(barrier, inc=1, device_id=device, device_id_type=pl.DeviceIdType.MESH)
 
@@ -104,13 +104,23 @@
     def toward(name, k, part):
         send(msg, (name, k), part, at(-flip * k if name == "urgent" else flip * k))
 
-    for i, k in enumerate(reaches):
-        pl.semaphore_signal(ready.at[i], inc=1, device_id=at(-flip * k), device_id_type=pl.DeviceIdType.MESH)
     for part in every:
         for k in reaches:
-            toward("urgent", k, part)
+            send(msg, ("urgent", k), part, at(-flip * k), False)
+            send(msg, ("plain", k), part, at(flip * k), False)
+
+    def start(order):
+        for name, part in order:
+            for k in reaches:
+                copies[(name, k), part].start()
+
+    start([("urgent", part) for part in every])
+    for part in every:
         send(msg, "mate", part, mate)
+    for part in every:
         send(msg, "partner", part, partner)
+    start([("plain", part) for part in every])
+
     dim = lax.broadcasted_iota(jnp.int32, (dims, 128), 0)
     length = jnp.full((dims, 128), 1.0, f32)
     for d in range(dims):
@@ -183,22 +193,20 @@
     for part in every:
         land("partner", part)
     visit(*[("partner", part) for part in every])
-    for i, k in enumerate(reaches):
-        pl.semaphore_wait(ready.at[i], 1)
-        for part in every:
-            toward("plain", k, part)
-
     last = steps
     inner = [(name, k) for k in reaches if k < last for name in ("urgent", "plain")]
     urgent, plain = ("urgent", last), ("plain", last)
     cross = jnp.where(core == side, slot(urgent), slot(plain))
     for part in every:
         land("mate", part, "mate2", partner)
-        visit(("mate", part))
-    for part in every:
         land(urgent, part, "over", mate)
-        land("mate2", part)
-        visit(("mate2", part), (urgent, part))
+        if part:
+            land("mate2", part - 1)
+            visit(("mate2", part - 1), ("mate", part), (urgent, part))
+        else:
+            visit(("mate", part), (urgent, part))
+    land("mate2", parts - 1)
+    visit(("mate2", parts - 1))
     for one in inner:
         for part in every:
             land(one, part, ("over", one), mate)
@@ -207,7 +215,15 @@
     for part in every:
         land(plain, part, "cross", partner, cross)
         land("over", part, "over2", partner)
-        visit((plain, part), ("over", part))
+        if part:
+            land("cross", part - 1)
+            land("over2", part - 1)
+            visit((plain, part), ("over", part), ("cross", part - 1), ("over2", part - 1))
+        else:
+            visit((plain, part), ("over", part))
+    land("cross", parts - 1)
+    land("over2", parts - 1)
+    visit(("cross", parts - 1), ("over2", parts - 1))
     for one in inner:
         for part in every:
             land(("over", one), part, ("over2", one), partner)
@@ -215,10 +231,6 @@
             visit((("over", one), part), (("core", one), part))
             land(("over2", one), part)
             visit((("over2", one), part))
-    for part in every:
-        land("cross", part)
-        land("over2", part)
-        visit(("cross", part), ("over2", part))
     settle()
     total = acc[...]
     moved = total[:dims] + total[dims : 2 * dims] + total[2 * dims : 3 * dims]
@@ -256,7 +268,6 @@
             pltpu.VMEM((chunk, piece), f32),
             pltpu.VMEM((3 * dims + 16, block), f32),
             pltpu.SemaphoreType.DMA((parts + 4,)),
-            pltpu.SemaphoreType.REGULAR((steps // 4,)),
             pltpu.SemaphoreType.DMA((2 * steps, parts)),
             pltpu.SemaphoreType.DMA((2 * steps, parts)),
         ],

time: 23 us -> 21.6 us (0.939)
  Pallas kernels: 22.1 us -> 20.7 us
    pallas_call x1, Pallas kernels: 22.1 us -> 20.7 us  [on_device(): pl.pallas_call(functools.partial(kernel, dims, steps, count), out_shape=p...]
where the time goes in v2:
time: 21.6 us; the launch traced here: 21.4 us
  Pallas kernels  20.7 us (96%)
  local copies, waits for them, and re-layouts  0.64 us (3%)
    pallas_call x1, Pallas kernels, on_device(): pl.pallas_call(functools.partial(kernel, dims, steps, count), out_shape=p...  20.7 us
    unnamed x1, local copies, waits for them, and re-layouts  0.64 us

profile of v2, /device:TPU:0, one launch (start us, length us, event | category | flops | bytes accessed | tf_op | source)
XLA Modules:
  0.0 21.4 jit_solution(1454211631630504891)
XLA Ops:
  0.0 20.7 %shard_map.55 = f32[32,768]{1,0:T(8,128)S(1)} custom-call(f32[32,768]{1,0:T(8,128)} %coords.1, f32[768]{0:T(1024)} %alpha.1, f32[15,768]{1,0:T(8,128)} %solves.1, f32[15,768]{1,0:T(8,128)} %probes.1, f32[32]{0:T(128)} %lengths.1), custom_call_target="tpu_custom_call" | custom-call | tf_op jit(solution)/shard_map/pallas_call | solution.py:251
  20.7 0.6 %copy.7 = f32[32,768]{1,0:T(8,128)} copy(f32[32,768]{1,0:T(8,128)S(1)} %shard_map.55) | data formatting | bytes 196608

commit v3 on v2

--- a/solution.py
+++ b/solution.py
@@ -36,7 +36,7 @@
 
 def kernel(
     dims, steps, count, coords, alpha, solves, probes, lengths, out,
-    msg, line, held, held2, scales, recv, left_d, left_c, right_d, right_c, hold_d, hold_c, acc, load_sem, send_sem, recv_sem,
+    msg, line, held, held2, scales, recv, left_d, left_c, right_d, right_c, hold_d, hold_c, acc, load_sem, ready, send_sem, recv_sem,
 ):
     me = lax.axis_index("blk")
     core = lax.rem(me, 2)
@@ -53,7 +53,7 @@
     reaches = range(4, steps + 1, 4)
     barrier = pltpu.get_barrier_semaphore()
     flip = 1 - 2 * side
-    devices = [at(sign * k) for k in reaches for sign in (1, -1)] + [mate, partner]
+    devices = [at(flip * k) for k in reaches] + [mate, partner]
     for device in devices:
         pl.semaphore_signal(barrier, inc=1, device_id=device, device_id_type=pl.DeviceIdType.MESH)
 
@@ -83,7 +83,7 @@
             names.append(name)
         return names.index(name)
 
-    def send(src, name, part, device, now=True):
+    def send(src, name, part, device):
         copy = pltpu.make_async_remote_copy(
             src_ref=src.at[part],
             dst_ref=recv.at[slot(name), part],
@@ -92,8 +92,7 @@
             device_id=device,
             device_id_type=pl.DeviceIdType.MESH,
         )
-        if now:
-            copy.start()
+        copy.start()
         copies[name, part] = copy
 
     def arrive(name, part):
@@ -101,25 +100,14 @@
 
     every = range(parts)
 
-    def toward(name, k, part):
-        send(msg, (name, k), part, at(-flip * k if name == "urgent" else flip * k))
-
+    for i, k in enumerate(reaches):
+        pl.semaphore_signal(ready.at[i], inc=1, device_id=at(-flip * k), device_id_type=pl.DeviceIdType.MESH)
     for part in every:
         for k in reaches:
-            send(msg, ("urgent", k), part, at(-flip * k), False)
-            send(msg, ("plain", k), part, at(flip * k), False)
-
-    def start(order):
-        for name, part in order:
-            for k in reaches:
-                copies[(name, k), part].start()
-
-    start([("urgent", part) for part in every])
-    for part in every:
+            send(msg, ("urgent", k), part, at(-flip * k))
         send(msg, "mate", part, mate)
     for part in every:
         send(msg, "partner", part, partner)
-    start([("plain", part) for part in every])
 
     dim = lax.broadcasted_iota(jnp.int32, (dims, 128), 0)
     length = jnp.full((dims, 128), 1.0, f32)
@@ -176,8 +164,8 @@
             right_c[buffer] = jnp.concatenate([high, mid, low, high, mid, high], 0)
             for start in range(0, block, chunk):
                 lines = pl.ds(start, chunk)
+                coupling = jnp.dot(left_c[lines, :], right_c[buffer], preferred_element_type=f32)
                 distance = jnp.dot(left_d[lines, :], right_d[buffer], preferred_element_type=f32)
-                coupling = jnp.dot(left_c[lines, :], right_c[buffer], preferred_element_type=f32)
                 if start + chunk == block and (name, part) == tiles[-1]:
                     hold_d[...] = distance
                     hold_c[...] = coupling
@@ -193,6 +181,10 @@
     for part in every:
         land("partner", part)
     visit(*[("partner", part) for part in every])
+    for i, k in enumerate(reaches):
+        pl.semaphore_wait(ready.at[i], 1)
+        for part in every:
+            send(msg, ("plain", k), part, at(flip * k))
     last = steps
     inner = [(name, k) for k in reaches if k < last for name in ("urgent", "plain")]
     urgent, plain = ("urgent", last), ("plain", last)
@@ -213,8 +205,8 @@
             send(recv.at[slot(one)], ("core", one), part, partner)
             visit((one, part))
     for part in every:
+        land("over", part, "over2", partner)
         land(plain, part, "cross", partner, cross)
-        land("over", part, "over2", partner)
         if part:
             land("cross", part - 1)
             land("over2", part - 1)
@@ -268,6 +260,7 @@
             pltpu.VMEM((chunk, piece), f32),
             pltpu.VMEM((3 * dims + 16, block), f32),
             pltpu.SemaphoreType.DMA((parts + 4,)),
+            pltpu.SemaphoreType.REGULAR((steps // 4,)),
             pltpu.SemaphoreType.DMA((2 * steps, parts)),
             pltpu.SemaphoreType.DMA((2 * steps, parts)),
         ],

time: 21.6 us -> 21.1 us (0.977)
  Pallas kernels: 20.7 us -> 20.2 us
    pallas_call x1, Pallas kernels: 20.7 us -> 20.2 us  [on_device(): pl.pallas_call(functools.partial(kernel, dims, steps, count), out_shape=p...]
where the time goes in v3:
time: 21.1 us; the launch traced here: 20.9 us
  Pallas kernels  20.2 us (96%)
  local copies, waits for them, and re-layouts  0.64 us (3%)
    pallas_call x1, Pallas kernels, on_device(): pl.pallas_call(functools.partial(kernel, dims, steps, count), out_shape=p...  20.2 us
    unnamed x1, local copies, waits for them, and re-layouts  0.64 us

profile of v3, /device:TPU:0, one launch (start us, length us, event | category | flops | bytes accessed | tf_op | source)
XLA Modules:
  0.0 20.9 jit_solution(16786398987182077285)
XLA Ops:
  0.0 20.2 %shard_map.55 = f32[32,768]{1,0:T(8,128)S(1)} custom-call(f32[32,768]{1,0:T(8,128)} %coords.1, f32[768]{0:T(1024)} %alpha.1, f32[15,768]{1,0:T(8,128)} %solves.1, f32[15,768]{1,0:T(8,128)} %probes.1, f32[32]{0:T(128)} %lengths.1), custom_call_target="tpu_custom_call" | custom-call | tf_op jit(solution)/shard_map/pallas_call | solution.py:243
  20.2 0.6 %copy.7 = f32[32,768]{1,0:T(8,128)} copy(f32[32,768]{1,0:T(8,128)S(1)} %shard_map.55) | data formatting | bytes 196608

commit v4 on v3

--- a/solution.py
+++ b/solution.py
@@ -12,7 +12,7 @@
 ln_two = math.log(2.0)
 inv_ln_two = 1.0 / ln_two
 f32, bf16 = jnp.float32, jnp.bfloat16
-piece, chunk = 256, 128
+piece, chunk, kept = 256, 128, 2
 
 
 def pieces(x):
@@ -148,8 +148,9 @@
             acc[:, lines] += part_sum
 
     def settle():
-        if pending:
-            finish(hold_d[...], hold_c[...], *pending.pop())
+        while pending:
+            which, *rest = pending.pop(0)
+            finish(hold_d[which], hold_c[which], *rest)
 
     def visit(*tiles):
         settle()
@@ -166,10 +167,11 @@
                 lines = pl.ds(start, chunk)
                 coupling = jnp.dot(left_c[lines, :], right_c[buffer], preferred_element_type=f32)
                 distance = jnp.dot(left_d[lines, :], right_d[buffer], preferred_element_type=f32)
-                if start + chunk == block and (name, part) == tiles[-1]:
-                    hold_d[...] = distance
-                    hold_c[...] = coupling
-                    pending.append((buffer, lines, fresh))
+                which = (block - start) // chunk - 1
+                if which < kept and (name, part) == tiles[-1]:
+                    hold_d[which] = distance
+                    hold_c[which] = coupling
+                    pending.append((which, buffer, lines, fresh))
                 else:
                     finish(distance, coupling, buffer, lines, fresh)
 
@@ -256,8 +258,8 @@
             pltpu.VMEM((block, depth_c), bf16),
             pltpu.VMEM((2, depth_d, piece), bf16),
             pltpu.VMEM((2, depth_c, piece), bf16),
-            pltpu.VMEM((chunk, piece), f32),
-            pltpu.VMEM((chunk, piece), f32),
+            pltpu.VMEM((kept, chunk, piece), f32),
+            pltpu.VMEM((kept, chunk, piece), f32),
             pltpu.VMEM((3 * dims + 16, block), f32),
             pltpu.SemaphoreType.DMA((parts + 4,)),
             pltpu.SemaphoreType.REGULAR((steps // 4,)),

time: 21.1 us -> 20.8 us (0.986)
    pallas_call x1, Pallas kernels: 20.2 us -> 20 us  [on_device(): pl.pallas_call(functools.partial(kernel, dims, steps, count), out_shape=p...]
where the time goes in v4:
time: 20.8 us; the launch traced here: 20.6 us
  Pallas kernels  20 us (96%)
  local copies, waits for them, and re-layouts  0.64 us (3%)
    pallas_call x1, Pallas kernels, on_device(): pl.pallas_call(functools.partial(kernel, dims, steps, count), out_shape=p...  20 us
    unnamed x1, local copies, waits for them, and re-layouts  0.64 us

profile of v4, /device:TPU:0, one launch (start us, length us, event | category | flops | bytes accessed | tf_op | source)
XLA Modules:
  0.0 20.6 jit_solution(17239885419672097002)
XLA Ops:
  0.0 20.0 %shard_map.55 = f32[32,768]{1,0:T(8,128)S(1)} custom-call(f32[32,768]{1,0:T(8,128)} %coords.1, f32[768]{0:T(1024)} %alpha.1, f32[15,768]{1,0:T(8,128)} %solves.1, f32[15,768]{1,0:T(8,128)} %probes.1, f32[32]{0:T(128)} %lengths.1), custom_call_target="tpu_custom_call" | custom-call | tf_op jit(solution)/shard_map/pallas_call | solution.py:245
  20.0 0.6 %copy.7 = f32[32,768]{1,0:T(8,128)} copy(f32[32,768]{1,0:T(8,128)S(1)} %shard_map.55) | data formatting | bytes 196608
